TPU v7x, 32 devices: a whole 2x2x4 slice. The times are simulated.
32 devices in a mesh: mem: 8 (over y, x, core), patch: 4 (over z).
Axes of the slice: x: 2, y: 2, z: 4, core: 2. Of those that a mesh axis runs over, the one named last changes fastest.
Arguments:
- state: bfloat16 [1024, 16384], P('mem', 'patch'), may hold values from -6 to 6
- obs_ens: bfloat16 [1024, 8192], P('mem', 'patch'), may hold values from -6 to 6
- obs_values: float32 [8192], P('patch'), may hold values from -8 to 8
- obs_weight: float32 [8192], P('patch'), may hold values from 0.2 to 5
- counts: int32 [32], P('patch'), may hold values from 32 to 256
Outputs:
- analysis: bfloat16 [1024, 16384], P('mem', 'patch')
Inputs may be any that keep to these rules, and one draw needn't show every extreme that they name: Region r uses the first counts[r] of its 256 observations.
All inputs are finite; a program needn't handle non-finite values. Where the computation divides by a largest or mean magnitude, that divisor is 1e-20 or more.
Results may differ from a plain program's by a relative error of at most 0.0047.
Values may be sent and summed in bfloat16 or wider, within the bound.
A program may use at most 64 MiB of HBM per device.

v0:
```python
import math
import jax
import jax.numpy as jnp
from jax import lax
from jax.sharding import PartitionSpec as P

DEGREE = 7


def extended(cells, sides, width):
    for axis, dim in sides:
        count = lax.axis_size(axis)
        head = lax.slice_in_dim(cells, 0, width, axis=dim)
        tail = lax.slice_in_dim(cells, cells.shape[dim] - width, cells.shape[dim], axis=dim)
        cells = jnp.concatenate(
            [
                lax.ppermute(tail, axis, [(i, (i + 1) % count) for i in range(count)]),
                cells,
                lax.ppermute(head, axis, [((i + 1) % count, i) for i in range(count)]),
            ],
            axis=dim,
        )
    return cells


def root_curve(values):
    lifted = jnp.sqrt(1.0 + values)
    return -1.0 / (lifted * (1.0 + lifted))


def inverse_curve(values):
    return 1.0 / (1.0 + values)


def chebyshev(upper, curve):
    number = DEGREE + 1
    theta = (jnp.arange(number, dtype=jnp.float32) + 0.5) * (math.pi / number)
    nodes = upper * (jnp.cos(theta) + 1.0) * 0.5
    samples = curve(nodes)
    orders = jnp.arange(number, dtype=jnp.float32)
    table = jnp.cos(orders[:, None] * theta[None, :])
    coefs = 2.0 / number * jnp.sum(table * samples[None, :], axis=1)
    return coefs * jnp.where(orders == 0.0, 0.5, 1.0)


def clenshaw(block, matrix, coefs):
    nearer = coefs[DEGREE] * block
    farther = jnp.zeros_like(block)
    for order in range(DEGREE - 1, 0, -1):
        current = (
            coefs[order] * block
            + 2.0 * jnp.dot(nearer, matrix, precision=lax.Precision.HIGHEST)
            - farther
        )
        farther, nearer = (nearer, current)
    return coefs[0] * block + jnp.dot(nearer, matrix, precision=lax.Precision.HIGHEST) - farther


def cross_product(left, right):
    return lax.dot_general(
        left, right, (((0,), (0,)), ((), ())), preferred_element_type=jnp.float32
    )


def on_device(state, obs_ens, obs_values, obs_weight, counts):
    mem_index = lax.axis_index("mem")
    own = obs_ens.shape[1] // lax.axis_size("mem")
    half = own // 2
    values = lax.dynamic_slice_in_dim(obs_values, mem_index * own, own, 0)
    weights = lax.dynamic_slice_in_dim(obs_weight, mem_index * own, own, 0)
    count = lax.dynamic_slice_in_dim(counts, mem_index, 1, 0)[0]
    region_state, region_obs = (
        lax.all_to_all(state, "mem", split_axis=1, concat_axis=0, tiled=True),
        lax.all_to_all(obs_ens, "mem", split_axis=1, concat_axis=0, tiled=True),
    )
    members = region_obs.shape[0]
    full_obs = region_obs.astype(jnp.float32)
    obs_centre = jnp.mean(full_obs, axis=0)
    mask = (jnp.arange(own, dtype=jnp.int32) < count).astype(jnp.float32)
    root = jnp.sqrt(weights * mask)
    own_gains = ((full_obs - obs_centre[None, :]) * root[None, :]).astype(jnp.bfloat16)
    own_innov = (root * (values - obs_centre)).astype(jnp.bfloat16)
    stacked = jnp.concatenate([own_gains, own_innov[None, :]], axis=0)
    widened = extended(stacked, (("patch", 1),), half)
    gains = widened[:-1]
    innov = widened[-1].astype(jnp.float32)
    normal = cross_product(gains, gains) / (members - 1)
    upper = jnp.max(jnp.sum(jnp.abs(normal), axis=1)) + 1e-06
    shifted = normal * (2.0 / upper) - jnp.eye(normal.shape[0], dtype=jnp.float32)
    full = region_state.astype(jnp.float32)
    centre = jnp.mean(full, axis=0)
    spread = (full - centre[None, :]).astype(jnp.bfloat16)
    product = cross_product(spread, gains)
    mixed = clenshaw(product, shifted, chebyshev(upper, root_curve)).astype(jnp.bfloat16)
    mean_weights = clenshaw(innov[None, :], shifted, chebyshev(upper, inverse_curve))[0]
    mean_shift = jnp.dot(product, mean_weights, precision=lax.Precision.HIGHEST) / (members - 1)
    update = lax.dot_general(
        gains, mixed, (((1,), (1,)), ((), ())), preferred_element_type=jnp.float32
    ) / (members - 1)
    analysed = (full + mean_shift[None, :] + update).astype(jnp.bfloat16)
    return lax.all_to_all(analysed, "mem", split_axis=0, concat_axis=1, tiled=True)


def solution(mesh):
    placed = (P("mem", "patch"), P("mem", "patch"), P("patch"), P("patch"), P("patch"))
    return jax.shard_map(
        on_device, mesh=mesh, in_specs=placed, out_specs=P("mem", "patch"), check_vma=False
    )
```

profile of v0, /device:TPU:0, one launch (start us, length us, event | category | flops | bytes accessed | tf_op | source)
XLA Modules:
  0.0 93.4 jit_solution(3490035947268976717)
XLA Ops:
  0.0 2.1 %copy.15 = bf16[128,2048]{0,1:T(8,128)(2,1)} copy(bf16[128,2048]{1,0:T(8,128)(2,1)} %param.6) | data formatting | bytes 1048576 | tf_op args[1]
  2.1 5.2 %all-to-all-start.1 = ((bf16[128,8,256]{0,2,1:T(8,128)(2,1)}), bf16[128,8,256]{0,2,1:T(8,128)(2,1)S(1)}, u32[]{:S(2)}, u32[]{:S(2)}) async-start(bf16[128,8,256]{0,2,1:T(8,128)(2,1)} %bitcast.3), calls=%async_computation.1 | async-start | bytes 1048576 | tf_op jit(solution)/shard_map/all_to_all | solution.py:74
  7.9 9.1 %all-to-all-done.1 = bf16[128,8,256]{0,2,1:T(8,128)(2,1)S(1)} async-done(((bf16[128,8,256]{0,2,1:T(8,128)(2,1)}), bf16[128,8,256]{0,2,1:T(8,128)(2,1)S(1)}, u32[]{:S(2)}, u32[]{:S(2)}) %all-to-all-start.1) | async-done | bytes 524320 | tf_op jit(solution)/shard_map/all_to_all | solution.py:74
  17.1 1.4 %multiply_convert_fusion = (bf16[256]{0:T(256)(128)(2,1)S(1)}, f32[256]{0:T(256)S(1)}, f32[256]{0:T(256)S(1)}) fusion(f32[2048]{0:T(1024)} %param.7, s32[]{:T(128)S(6)} %select_n.15, f32[256]{0:T(256)S(1)} %convert_reduce_fusion.1, f32[2048]{0:T(1024)} %param.8, s32[]{:T(128)} %bitcast.6), kind=kLoop, calls=%fused_computation.72 | loop fusion | flops 1536 | bytes 5640 | tf_op jit(solution)/shard_map/convert_element_type | solution.py:82
  19.1 1.6 %collective-permute-start = (bf16[1025,128]{1,0:T(8,128)(2,1)S(1)}, bf16[1025,128]{1,0:T(8,128)(2,1)S(1)}, u32[]{:S(2)}, u32[]{:S(2)}) collective-permute-start(bf16[1025,128]{1,0:T(8,128)(2,1)S(1)} %get-tuple-element.11), channel_id=1, source_target_pairs={{0,1},{1,2},{2,3},{3,0},{4,5},{5,6},{6,7},{7,4},{8,9},{9,10},{10,1... | collective-permute-start | bytes 787208 | tf_op jit(solution)/shard_map/ppermute | solution.py:17
  20.8 2.2 %collective-permute-start.1 = (bf16[1025,128]{1,0:T(8,128)(2,1)S(1)}, bf16[1025,128]{1,0:T(8,128)(2,1)S(1)}, u32[]{:S(2)}, u32[]{:S(2)}) collective-permute-start(bf16[1025,128]{1,0:T(8,128)(2,1)S(1)} %get-tuple-element.12), channel_id=1, source_target_pairs={{1,0},{2,1},{3,2},{0,3},{5,4},{6,5},{7,6},{4,7},{9,8},{10,9},{11,1... | collective-permute-start | bytes 787208 | tf_op jit(solution)/shard_map/ppermute | solution.py:19
  23.0 1.1 %copy.21 = bf16[16,8,8,512]{3,2,0,1:T(8,128)(2,1)} copy(bf16[16,8,8,512]{3,2,1,0:T(8,128)(2,1)S(1)} %bitcast.86) | data formatting | bytes 2097152 | tf_op jit(solution)/shard_map/all_to_all | solution.py:73
  24.1 3.6 %all-to-all-start = ((bf16[128,8,512]{2,0,1:T(8,128)(2,1)}), bf16[128,8,512]{2,0,1:T(8,128)(2,1)S(1)}, u32[]{:S(2)}, u32[]{:S(2)}) async-start(bf16[128,8,512]{2,0,1:T(8,128)(2,1)} %bitcast.83), calls=%async_computation | async-start | bytes 2097152 | tf_op jit(solution)/shard_map/all_to_all | solution.py:73
  27.7 2.1 %collective-permute-done = bf16[1025,128]{1,0:T(8,128)(2,1)S(1)} collective-permute-done((bf16[1025,128]{1,0:T(8,128)(2,1)S(1)}, bf16[1025,128]{1,0:T(8,128)(2,1)S(1)}, u32[]{:S(2)}, u32[]{:S(2)}) %collective-permute-start) | collective-permute-done | bytes 262432 | tf_op jit(solution)/shard_map/ppermute | solution.py:17
  29.8 2.2 %collective-permute-done.1 = bf16[1025,128]{1,0:T(8,128)(2,1)S(1)} collective-permute-done((bf16[1025,128]{1,0:T(8,128)(2,1)S(1)}, bf16[1025,128]{1,0:T(8,128)(2,1)S(1)}, u32[]{:S(2)}, u32[]{:S(2)}) %collective-permute-start.1) | collective-permute-done | bytes 262432 | tf_op jit(solution)/shard_map/ppermute | solution.py:19
  36.8 4.4 %broadcast_multiply_fusion.8 = (f32[1,512]{1,0:T(1,128)S(1)}, f32[1,512]{1,0:T(1,128)S(1)}, f32[1,512]{1,0:T(1,128)S(1)}, f32[1,512]{1,0:T(1,128)S(1)}, f32[1,51...) fusion(f32[1,512]{1,0:T(1,128)S(1)} %get-tuple-element.8, f32[]{:T(128)} %bitcast.7, f32[]{:T(128)} %bitcast.19, ...), kind=kLoop, calls=%fused_computation.71 | loop fusion | flops 3584 | bytes 16412 | tf_op jit(solution)/shard_map/mul | solution.py:56
  43.1 1.0 %fusion.31 = f32[1,512]{1,0:T(1,128)S(1)} fusion(f32[512,1]{0,1:T(1,128)S(1)} %bitcast.91, f32[512,512]{0,1:T(8,128)S(1)} %get-tuple-element.38, f32[]{:T(128)S(6)} %mul.339), kind=kOutput, calls=%fused_computation.86 | convolution fusion | flops 4194304 | bytes 1052676 | tf_op jit(solution)/shard_map/dot_general | solution.py:52
  48.4 1.0 %copy-done.1 = bf16[1025,512]{1,0:T(8,128)(2,1)S(1)} copy-done((bf16[1025,512]{1,0:T(8,128)(2,1)S(1)}, bf16[1025,512]{1,0:T(8,128)(2,1)}, u32[]{:S(2)}) %copy-start.1) | copy-done | bytes 1049624
  50.2 1.0 %fusion.36 = f32[1,512]{1,0:T(1,128)S(1)} fusion(f32[512,512]{1,0:T(8,128)S(1)} %fusion.15, f32[512,1]{0,1:T(1,128)S(1)} %bitcast.96), kind=kOutput, calls=%fused_computation.90 | convolution fusion | flops 3145728 | bytes 1052672 | tf_op jit(solution)/shard_map/dot_general | solution.py:96
  51.2 3.2 %multiply_add_fusion = f32[512,512]{1,0:T(8,128)S(1)} fusion(f32[512,512]{1,0:T(8,128)S(1)} %fusion.15, f32[]{:T(128)} %bitcast.46, f32[]{:T(128)} %bitcast.45, f32[512,512]{0,1:T(8,128)S(1)} %get-tuple-element.38, f32[]{:T(128)S(6)} %mul.339), kind=kOutput, calls=%fused_computation.27 | convolution fusion | flops 1612709888 | bytes 3145740 | tf_op jit(solution)/shard_map/dot_general | solution.py:52
  54.4 1.9 %convolution_multiply_fusion.4 = f32[512,512]{1,0:T(8,128)S(1)} fusion(f32[512,512]{1,0:T(8,128)S(1)} %multiply_add_fusion, f32[512,512]{0,1:T(8,128)S(1)} %get-tuple-element.38, f32[]{:T(128)S(6)} %mul.339), kind=kOutput, calls=%fused_computation.10 | convolution fusion | flops 1611923456 | bytes 3145732 | tf_op jit(solution)/shard_map/dot_general | solution.py:52
  56.3 4.1 %add_subtract_fusion.2 = f32[512,512]{1,0:T(8,128)S(1)} fusion(f32[512,512]{1,0:T(8,128)S(1)} %multiply_add_fusion, f32[512,512]{1,0:T(8,128)S(1)} %fusion.15, f32[512,512]{1,0:T(8,128)S(1)} %convolution_multiply_fusion.4, f32[]{:T(128)} %bitcast.46, f32[]{:T(128)} %bitcast.44, f32[]{:T(128)} %bitcast.43, f32[512,512]{0,1:T(8,128)S(1)} %get-tuple-element.38, ...), kind=kOutput, calls=%fused_computation.25 | convolution fusion | flops 1613758464 | bytes 5242896 | tf_op jit(solution)/shard_map/dot_general | solution.py:52
  60.4 3.9 %add_subtract_fusion.1 = f32[512,512]{1,0:T(8,128)S(1)} fusion(f32[512,512]{1,0:T(8,128)S(1)} %fusion.15, f32[512,512]{1,0:T(8,128)S(1)} %convolution_multiply_fusion.4, f32[512,512]{1,0:T(8,128)S(1)} %add_subtract_fusion.2, f32[]{:T(128)} %bitcast.46, f32[]{:T(128)} %bitcast.44, f32[]{:T(128)} %bitcast.42, f32[512,512]{0,1:T(8,128)S(1)} %get-tuple-element.38, ...), kind=kOutput, calls=%fused_computation.24 | convolution fusion | flops 1613758464 | bytes 5242896 | tf_op jit(solution)/shard_map/dot_general | solution.py:52
  64.3 2.6 %add_subtract_fusion = f32[512,512]{1,0:T(8,128)S(1)} fusion(f32[512,512]{1,0:T(8,128)S(1)} %add_subtract_fusion.2, f32[512,512]{1,0:T(8,128)S(1)} %fusion.15, f32[512,512]{1,0:T(8,128)S(1)} %add_subtract_fusion.1, f32[]{:T(128)} %bitcast.41, f32[512,512]{0,1:T(8,128)S(1)} %get-tuple-element.38, f32[]{:T(128)S(6)} %mul.339), kind=kOutput, calls=%fused_computation.23 | convolution fusion | flops 1612709888 | bytes 5242888 | tf_op jit(solution)/shard_map/dot_general | solution.py:52
  66.9 1.9 %convolution_multiply_fusion = f32[512,512]{1,0:T(8,128)S(1)} fusion(f32[512,512]{1,0:T(8,128)S(1)} %add_subtract_fusion, f32[512,512]{0,1:T(8,128)S(1)} %get-tuple-element.38, f32[]{:T(128)S(6)} %mul.339), kind=kOutput, calls=%fused_computation.6 | convolution fusion | flops 1611923456 | bytes 3145732 | tf_op jit(solution)/shard_map/dot_general | solution.py:52
  68.8 2.6 %fusion.5 = f32[512,512]{1,0:T(8,128)S(1)} fusion(f32[512,512]{1,0:T(8,128)S(1)} %add_subtract_fusion.1, f32[512,512]{1,0:T(8,128)S(1)} %convolution_multiply_fusion, f32[512,512]{1,0:T(8,128)S(1)} %fusion.15, f32[]{:T(128)} %bitcast.40, f32[512,512]{0,1:T(8,128)S(1)} %get-tuple-element.38, f32[]{:T(128)S(6)} %mul.339), kind=kOutput, calls=%fused_computation.20 | convolution fusion | flops 1612447744 | bytes 5242888 | tf_op jit(solution)/shard_map/dot_general | solution.py:56
  71.4 1.4 %fusion.2 = bf16[1024,512]{1,0:T(8,128)(2,1)S(1)} fusion(bf16[128,8,512]{2,0,1:T(8,128)(2,1)S(1)} %all-to-all-done, f32[512]{0:T(512)S(1)} %broadcast_multiply_fusion, bf16[1025,512]{1,0:T(8,128)(2,1)S(1)} %copy-done.1, f32[512,512]{1,0:T(8,128)S(1)} %add_subtract_fusion, f32[512,512]{1,0:T(8,128)S(1)} %fusion.5, f32[512,512]{1,0:T(8,128)S(1)} %fusion.15, ...), kind=kOutput, calls=%fused_computation.5 | convolution fusion | flops 540540928 | bytes 6293508 | tf_op jit(solution)/shard_map/dot_general | solution.py:97
  72.9 19.5 %all_to_all.45 = bf16[8,128,512]{2,1,0:T(8,128)(2,1)S(1)} all-to-all(bf16[8,128,512]{2,1,0:T(8,128)(2,1)S(1)} %bitcast.85), channel_id=1, replica_groups=mesh['mem'=8,'patch'=4] {'mem'}, dimensions={0} | all-to-all | bytes 2097152 | tf_op jit(solution)/shard_map/all_to_all | solution.py:101
  92.3 1.1 %copy.19 = bf16[8,16,8,512]{3,2,0,1:T(8,128)(2,1)} copy(bf16[8,16,8,512]{3,2,1,0:T(8,128)(2,1)S(1)} %bitcast.84) | data formatting | bytes 2097152 | tf_op jit(solution)/shard_map/all_to_all | solution.py:101
  (44 shorter events, 12.4 us)
Async XLA Ops:
  0.0 7.3 %copy-start.3 = (s32[8]{0:T(128)S(1)}, s32[8]{0:T(128)}, u32[]{:S(2)}) copy-start(s32[8]{0:T(128)} %param.9) | copy-start | bytes 100
  2.1 14.9 %all-to-all-start.1 = ((bf16[128,8,256]{0,2,1:T(8,128)(2,1)}), bf16[128,8,256]{0,2,1:T(8,128)(2,1)S(1)}, u32[]{:S(2)}, u32[]{:S(2)}) async-start(bf16[128,8,256]{0,2,1:T(8,128)(2,1)} %bitcast.3), calls=%async_computation.1 | async-start | bytes 1048576 | tf_op jit(solution)/shard_map/all_to_all | solution.py:74
  19.0 4.1 %copy-start.2 = (bf16[128,4096]{1,0:T(8,128)(2,1)S(1)}, bf16[128,4096]{1,0:T(8,128)(2,1)}, u32[]{:S(2)}) copy-start(bf16[128,4096]{1,0:T(8,128)(2,1)} %param.5) | copy-start | bytes 3145732
  19.1 10.6 %collective-permute-start = (bf16[1025,128]{1,0:T(8,128)(2,1)S(1)}, bf16[1025,128]{1,0:T(8,128)(2,1)S(1)}, u32[]{:S(2)}, u32[]{:S(2)}) collective-permute-start(bf16[1025,128]{1,0:T(8,128)(2,1)S(1)} %get-tuple-element.11), channel_id=1, source_target_pairs={{0,1},{1,2},{2,3},{3,0},{4,5},{5,6},{6,7},{7,4},{8,9},{9,10},{10,1... | collective-permute-start | bytes 787208 | tf_op jit(solution)/shard_map/ppermute | solution.py:17
  20.8 11.2 %collective-permute-start.1 = (bf16[1025,128]{1,0:T(8,128)(2,1)S(1)}, bf16[1025,128]{1,0:T(8,128)(2,1)S(1)}, u32[]{:S(2)}, u32[]{:S(2)}) collective-permute-start(bf16[1025,128]{1,0:T(8,128)(2,1)S(1)} %get-tuple-element.12), channel_id=1, source_target_pairs={{1,0},{2,1},{3,2},{0,3},{5,4},{6,5},{7,6},{4,7},{9,8},{10,9},{11,1... | collective-permute-start | bytes 787208 | tf_op jit(solution)/shard_map/ppermute | solution.py:19
  24.1 23.9 %all-to-all-start = ((bf16[128,8,512]{2,0,1:T(8,128)(2,1)}), bf16[128,8,512]{2,0,1:T(8,128)(2,1)S(1)}, u32[]{:S(2)}, u32[]{:S(2)}) async-start(bf16[128,8,512]{2,0,1:T(8,128)(2,1)} %bitcast.83), calls=%async_computation | async-start | bytes 2097152 | tf_op jit(solution)/shard_map/all_to_all | solution.py:73
  32.1 1.0 %copy-start = (bf16[1025,512]{1,0:T(8,128)(2,1)}, bf16[1025,512]{1,0:T(8,128)(2,1)S(1)}, u32[]{:S(2)}) copy-start(bf16[1025,512]{1,0:T(8,128)(2,1)S(1)} %pad_maximum_fusion) | copy-start | bytes 3148804
  48.2 1.2 %copy-start.1 = (bf16[1025,512]{1,0:T(8,128)(2,1)S(1)}, bf16[1025,512]{1,0:T(8,128)(2,1)}, u32[]{:S(2)}) copy-start(bf16[1025,512]{1,0:T(8,128)(2,1)} %copy-done) | copy-start | bytes 3148804
where the time goes:
time: 94 us; the launch traced here: 93.4 us
  matrix products  30.8 us (33%)
  blocking collectives  19.5 us (21%)
  waiting for transfers between devices  13.4 us (14%)
  starting transfers between devices  12.6 us (13%)
  other arithmetic  8.41 us (9%)
  local copies, waits for them, and re-layouts  7.73 us (8%)
    dot_general x14, matrix products, clenshaw(): jnp.dot(nearer, matrix, precision=lax.Precision.HIGHEST)  26.9 us
    all_to_all x1, blocking collectives, on_device(): lax.all_to_all(analysed, 'mem', split_axis=0, concat_axis=1, tiled=True)  19.5 us
    all_to_all x1, waiting for transfers between devices, on_device(): lax.all_to_all(obs_ens, 'mem', split_axis=1, concat_axis=0, tiled=True)  9.09 us
    all_to_all x1, starting transfers between devices, on_device(): lax.all_to_all(obs_ens, 'mem', split_axis=1, concat_axis=0, tiled=True)  5.2 us
    mul x1, other arithmetic, clenshaw(): coefs[0] * block + jnp.dot(nearer, matrix, precision=lax.Precision.HIGHEST)  4.4 us
    all_to_all x1, starting transfers between devices, on_device(): lax.all_to_all(state, 'mem', split_axis=1, concat_axis=0, tiled=True)  3.56 us
    unnamed x9, local copies, waits for them, and re-layouts  3.27 us
    ppermute x1, starting transfers between devices, extended(): lax.ppermute(head, axis, [((i + 1) % count, i) for i in range(count)])  2.25 us
  transfers between devices with their start and end apart: 4, of which 3 were waited for; matrix products, arithmetic and copies ran while one was open for 18% of the time, Pallas kernels for 0%

commit v1 on v0

--- a/solution.py
+++ b/solution.py
@@ -71,7 +71,12 @@
     count = lax.dynamic_slice_in_dim(counts, mem_index, 1, 0)[0]
     region_state, region_obs = (
         lax.all_to_all(state, "mem", split_axis=1, concat_axis=0, tiled=True),
-        lax.all_to_all(obs_ens, "mem", split_axis=1, concat_axis=0, tiled=True),
+        jnp.concatenate(
+            lax.all_to_all(
+                jnp.stack(jnp.split(obs_ens, lax.axis_size("mem"), axis=1)), "mem", 0, 0
+            ),
+            axis=0,
+        ),
     )
     members = region_obs.shape[0]
     full_obs = region_obs.astype(jnp.float32)

time: 94 us -> 104 us (1.11)
  local copies, waits for them, and re-layouts: 7.73 us -> 17.1 us
    unnamed x9 -> x15, local copies, waits for them, and re-layouts: 3.27 us -> 11.5 us
    another operation x0 -> x1, local copies, waits for them, and re-layouts: none -> 1.47 us  [on_device(): jnp.stack(jnp.split(obs_ens, lax.axis_size('mem'), axis=1))]
  transfers between devices with their start and end apart: 4 -> 4, of which waited for: 3 -> 3; matrix products, arithmetic and copies ran while one was open for 18% -> 16% of each run, Pallas kernels for 0% -> 0%
where the time goes in v1:
time: 104 us; the launch traced here: 103 us
  matrix products  30.9 us (30%)
  blocking collectives  19.4 us (19%)
  local copies, waits for them, and re-layouts  17.1 us (16%)
  waiting for transfers between devices  13.4 us (13%)
  starting transfers between devices  12.6 us (12%)
  other arithmetic  8.36 us (8%)
    dot_general x14, matrix products, clenshaw(): jnp.dot(nearer, matrix, precision=lax.Precision.HIGHEST)  26.9 us
    all_to_all x1, blocking collectives, on_device(): lax.all_to_all(analysed, 'mem', split_axis=0, concat_axis=1, tiled=True)  19.4 us
    unnamed x15, local copies, waits for them, and re-layouts  11.5 us
    all_to_all x1, waiting for transfers between devices, on_device(): lax.all_to_all(jnp.stack(jnp.split(obs_ens, lax.axis_size('mem'), axis=1)...  9.09 us
    all_to_all x1, starting transfers between devices, on_device(): lax.all_to_all(jnp.stack(jnp.split(obs_ens, lax.axis_size('mem'), axis=1)...  5.2 us
    mul x1, other arithmetic, clenshaw(): coefs[0] * block + jnp.dot(nearer, matrix, precision=lax.Precision.HIGHEST)  4.4 us
    all_to_all x1, starting transfers between devices, on_device(): lax.all_to_all(state, 'mem', split_axis=1, concat_axis=0, tiled=True)  3.56 us
    ppermute x1, starting transfers between devices, extended(): lax.ppermute(head, axis, [((i + 1) % count, i) for i in range(count)])  2.25 us
  transfers between devices with their start and end apart: 4, of which 3 were waited for; matrix products, arithmetic and copies ran while one was open for 16% of the time, Pallas kernels for 0%

profile of v1, /device:TPU:0, one launch (start us, length us, event | category | flops | bytes accessed | tf_op | source)
XLA Modules:
  0.0 102.7 jit_solution(5401994295244682768)
XLA Ops:
  0.0 1.5 %bitcast_dynamic-update-slice_fusion.7 = bf16[8,128,256]{2,1,0:T(8,128)(2,1)} fusion(bf16[128,2048]{1,0:T(8,128)(2,1)} %param.6), kind=kLoop, calls=%fused_computation.53 | loop fusion | bytes 131072
  1.5 1.5 %bitcast_dynamic-update-slice_fusion.6 = bf16[8,128,256]{2,1,0:T(8,128)(2,1)} fusion(bf16[8,128,256]{2,1,0:T(8,128)(2,1)} %bitcast_dynamic-update-slice_fusion.7, bf16[128,2048]{1,0:T(8,128)(2,1)} %param.6), kind=kLoop, calls=%fused_computation.52 | loop fusion | bytes 131072
  3.0 1.5 %bitcast_dynamic-update-slice_fusion.5 = bf16[8,128,256]{2,1,0:T(8,128)(2,1)} fusion(bf16[8,128,256]{2,1,0:T(8,128)(2,1)} %bitcast_dynamic-update-slice_fusion.6, bf16[128,2048]{1,0:T(8,128)(2,1)} %param.6), kind=kLoop, calls=%fused_computation.51 | loop fusion | bytes 131072
  4.4 1.5 %bitcast_dynamic-update-slice_fusion.4 = bf16[8,128,256]{2,1,0:T(8,128)(2,1)} fusion(bf16[8,128,256]{2,1,0:T(8,128)(2,1)} %bitcast_dynamic-update-slice_fusion.5, bf16[128,2048]{1,0:T(8,128)(2,1)} %param.6), kind=kLoop, calls=%fused_computation.50 | loop fusion | bytes 131072
  5.9 1.5 %bitcast_dynamic-update-slice_fusion.3 = bf16[8,128,256]{2,1,0:T(8,128)(2,1)} fusion(bf16[8,128,256]{2,1,0:T(8,128)(2,1)} %bitcast_dynamic-update-slice_fusion.4, bf16[128,2048]{1,0:T(8,128)(2,1)} %param.6), kind=kLoop, calls=%fused_computation.49 | loop fusion | bytes 131072
  7.4 1.5 %bitcast_dynamic-update-slice_fusion.2 = bf16[8,128,256]{2,1,0:T(8,128)(2,1)} fusion(bf16[8,128,256]{2,1,0:T(8,128)(2,1)} %bitcast_dynamic-update-slice_fusion.3, bf16[128,2048]{1,0:T(8,128)(2,1)} %param.6), kind=kLoop, calls=%fused_computation.48 | loop fusion | bytes 131072
  8.9 1.5 %bitcast_dynamic-update-slice_fusion.1 = bf16[8,128,256]{2,1,0:T(8,128)(2,1)} fusion(bf16[8,128,256]{2,1,0:T(8,128)(2,1)} %bitcast_dynamic-update-slice_fusion.2, bf16[128,2048]{1,0:T(8,128)(2,1)} %param.6), kind=kLoop, calls=%fused_computation.47 | loop fusion | bytes 131072
  10.3 1.5 %bitcast_dynamic-update-slice_fusion = bf16[8,128,256]{2,1,0:T(8,128)(2,1)} fusion(bf16[8,128,256]{2,1,0:T(8,128)(2,1)} %bitcast_dynamic-update-slice_fusion.1, bf16[128,2048]{1,0:T(8,128)(2,1)} %param.6), kind=kLoop, calls=%fused_computation.46 | loop fusion | bytes 131072 | tf_op jit(solution)/shard_map/stack | solution.py:76
  11.8 5.2 %all-to-all-start.1 = ((bf16[8,128,256]{2,1,0:T(8,128)(2,1)}), bf16[8,128,256]{2,1,0:T(8,128)(2,1)S(1)}, u32[]{:S(2)}, u32[]{:S(2)}) async-start(bf16[8,128,256]{2,1,0:T(8,128)(2,1)} %bitcast_dynamic-update-slice_fusion), calls=%async_computation.1 | async-start | bytes 1048576 | tf_op jit(solution)/shard_map/all_to_all | solution.py:75
  17.6 9.1 %all-to-all-done.1 = bf16[8,128,256]{2,1,0:T(8,128)(2,1)S(1)} async-done(((bf16[8,128,256]{2,1,0:T(8,128)(2,1)}), bf16[8,128,256]{2,1,0:T(8,128)(2,1)S(1)}, u32[]{:S(2)}, u32[]{:S(2)}) %all-to-all-start.1) | async-done | bytes 524320 | tf_op jit(solution)/shard_map/all_to_all | solution.py:75
  28.5 1.6 %collective-permute-start = (bf16[1025,128]{1,0:T(8,128)(2,1)S(1)}, bf16[1025,128]{1,0:T(8,128)(2,1)S(1)}, u32[]{:S(2)}, u32[]{:S(2)}) collective-permute-start(bf16[1025,128]{1,0:T(8,128)(2,1)S(1)} %get-tuple-element.11), channel_id=1, source_target_pairs={{0,1},{1,2},{2,3},{3,0},{4,5},{5,6},{6,7},{7,4},{8,9},{9,10},{10,1... | collective-permute-start | bytes 787208 | tf_op jit(solution)/shard_map/ppermute | solution.py:17
  30.1 2.2 %collective-permute-start.1 = (bf16[1025,128]{1,0:T(8,128)(2,1)S(1)}, bf16[1025,128]{1,0:T(8,128)(2,1)S(1)}, u32[]{:S(2)}, u32[]{:S(2)}) collective-permute-start(bf16[1025,128]{1,0:T(8,128)(2,1)S(1)} %get-tuple-element.12), channel_id=1, source_target_pairs={{1,0},{2,1},{3,2},{0,3},{5,4},{6,5},{7,6},{4,7},{9,8},{10,9},{11,1... | collective-permute-start | bytes 787208 | tf_op jit(solution)/shard_map/ppermute | solution.py:19
  33.4 3.6 %all-to-all-start = ((bf16[128,8,512]{2,0,1:T(8,128)(2,1)}), bf16[128,8,512]{2,0,1:T(8,128)(2,1)S(1)}, u32[]{:S(2)}, u32[]{:S(2)}) async-start(bf16[128,8,512]{2,0,1:T(8,128)(2,1)} %bitcast.96), calls=%async_computation | async-start | bytes 2097152 | tf_op jit(solution)/shard_map/all_to_all | solution.py:73
  37.0 2.1 %collective-permute-done = bf16[1025,128]{1,0:T(8,128)(2,1)S(1)} collective-permute-done((bf16[1025,128]{1,0:T(8,128)(2,1)S(1)}, bf16[1025,128]{1,0:T(8,128)(2,1)S(1)}, u32[]{:S(2)}, u32[]{:S(2)}) %collective-permute-start) | collective-permute-done | bytes 262432 | tf_op jit(solution)/shard_map/ppermute | solution.py:17
  39.1 2.2 %collective-permute-done.1 = bf16[1025,128]{1,0:T(8,128)(2,1)S(1)} collective-permute-done((bf16[1025,128]{1,0:T(8,128)(2,1)S(1)}, bf16[1025,128]{1,0:T(8,128)(2,1)S(1)}, u32[]{:S(2)}, u32[]{:S(2)}) %collective-permute-start.1) | collective-permute-done | bytes 262432 | tf_op jit(solution)/shard_map/ppermute | solution.py:19
  46.1 4.4 %broadcast_multiply_fusion.8 = (f32[1,512]{1,0:T(1,128)S(1)}, f32[1,512]{1,0:T(1,128)S(1)}, f32[1,512]{1,0:T(1,128)S(1)}, f32[1,512]{1,0:T(1,128)S(1)}, f32[1,51...) fusion(f32[1,512]{1,0:T(1,128)S(1)} %get-tuple-element.8, f32[]{:T(128)} %bitcast.13, f32[]{:T(128)} %bitcast.25, ...), kind=kLoop, calls=%fused_computation.78 | loop fusion | flops 3584 | bytes 16412 | tf_op jit(solution)/shard_map/mul | solution.py:56
  60.5 3.2 %multiply_add_fusion = f32[512,512]{1,0:T(8,128)S(1)} fusion(f32[512,512]{1,0:T(8,128)S(1)} %fusion.15, f32[]{:T(128)} %bitcast.52, f32[]{:T(128)} %bitcast.51, f32[512,512]{0,1:T(8,128)S(1)} %get-tuple-element.38, f32[]{:T(128)S(6)} %mul.339), kind=kOutput, calls=%fused_computation.25 | convolution fusion | flops 1612709888 | bytes 3145740 | tf_op jit(solution)/shard_map/dot_general | solution.py:52
  63.7 1.9 %convolution_multiply_fusion.4 = f32[512,512]{1,0:T(8,128)S(1)} fusion(f32[512,512]{1,0:T(8,128)S(1)} %multiply_add_fusion, f32[512,512]{0,1:T(8,128)S(1)} %get-tuple-element.38, f32[]{:T(128)S(6)} %mul.339), kind=kOutput, calls=%fused_computation.10 | convolution fusion | flops 1611923456 | bytes 3145732 | tf_op jit(solution)/shard_map/dot_general | solution.py:52
  65.6 4.1 %add_subtract_fusion.2 = f32[512,512]{1,0:T(8,128)S(1)} fusion(f32[512,512]{1,0:T(8,128)S(1)} %multiply_add_fusion, f32[512,512]{1,0:T(8,128)S(1)} %fusion.15, f32[512,512]{1,0:T(8,128)S(1)} %convolution_multiply_fusion.4, f32[]{:T(128)} %bitcast.52, f32[]{:T(128)} %bitcast.50, f32[]{:T(128)} %bitcast.49, f32[512,512]{0,1:T(8,128)S(1)} %get-tuple-element.38, ...), kind=kOutput, calls=%fused_computation.23 | convolution fusion | flops 1613758464 | bytes 5242896 | tf_op jit(solution)/shard_map/dot_general | solution.py:52
  69.8 3.9 %add_subtract_fusion.1 = f32[512,512]{1,0:T(8,128)S(1)} fusion(f32[512,512]{1,0:T(8,128)S(1)} %fusion.15, f32[512,512]{1,0:T(8,128)S(1)} %convolution_multiply_fusion.4, f32[512,512]{1,0:T(8,128)S(1)} %add_subtract_fusion.2, f32[]{:T(128)} %bitcast.52, f32[]{:T(128)} %bitcast.50, f32[]{:T(128)} %bitcast.48, f32[512,512]{0,1:T(8,128)S(1)} %get-tuple-element.38, ...), kind=kOutput, calls=%fused_computation.22 | convolution fusion | flops 1613758464 | bytes 5242896 | tf_op jit(solution)/shard_map/dot_general | solution.py:52
  73.7 2.6 %add_subtract_fusion = f32[512,512]{1,0:T(8,128)S(1)} fusion(f32[512,512]{1,0:T(8,128)S(1)} %add_subtract_fusion.2, f32[512,512]{1,0:T(8,128)S(1)} %fusion.15, f32[512,512]{1,0:T(8,128)S(1)} %add_subtract_fusion.1, f32[]{:T(128)} %bitcast.47, f32[512,512]{0,1:T(8,128)S(1)} %get-tuple-element.38, f32[]{:T(128)S(6)} %mul.339), kind=kOutput, calls=%fused_computation.21 | convolution fusion | flops 1612709888 | bytes 5242888 | tf_op jit(solution)/shard_map/dot_general | solution.py:52
  76.2 1.9 %convolution_multiply_fusion = f32[512,512]{1,0:T(8,128)S(1)} fusion(f32[512,512]{1,0:T(8,128)S(1)} %add_subtract_fusion, f32[512,512]{0,1:T(8,128)S(1)} %get-tuple-element.38, f32[]{:T(128)S(6)} %mul.339), kind=kOutput, calls=%fused_computation.6 | convolution fusion | flops 1611923456 | bytes 3145732 | tf_op jit(solution)/shard_map/dot_general | solution.py:52
  78.1 2.6 %fusion.5 = f32[512,512]{1,0:T(8,128)S(1)} fusion(f32[512,512]{1,0:T(8,128)S(1)} %add_subtract_fusion.1, f32[512,512]{1,0:T(8,128)S(1)} %convolution_multiply_fusion, f32[512,512]{1,0:T(8,128)S(1)} %fusion.15, f32[]{:T(128)} %bitcast.46, f32[512,512]{0,1:T(8,128)S(1)} %get-tuple-element.38, f32[]{:T(128)S(6)} %mul.339), kind=kOutput, calls=%fused_computation.18 | convolution fusion | flops 1612447744 | bytes 5242888 | tf_op jit(solution)/shard_map/dot_general | solution.py:56
  82.2 19.4 %all_to_all.37 = bf16[8,128,512]{2,1,0:T(8,128)(2,1)S(1)} all-to-all(bf16[8,128,512]{2,1,0:T(8,128)(2,1)S(1)} %bitcast.98), channel_id=1, replica_groups=mesh['mem'=8,'patch'=4] {'mem'}, dimensions={0} | all-to-all | bytes 2097152 | tf_op jit(solution)/shard_map/all_to_all | solution.py:106
  (49 shorter events, 20.0 us)
Async XLA Ops:
  0.0 17.0 %copy-start.3 = (s32[8]{0:T(128)S(1)}, s32[8]{0:T(128)}, u32[]{:S(2)}) copy-start(s32[8]{0:T(128)} %param.9) | copy-start | bytes 100
  11.8 14.9 %all-to-all-start.1 = ((bf16[8,128,256]{2,1,0:T(8,128)(2,1)}), bf16[8,128,256]{2,1,0:T(8,128)(2,1)S(1)}, u32[]{:S(2)}, u32[]{:S(2)}) async-start(bf16[8,128,256]{2,1,0:T(8,128)(2,1)} %bitcast_dynamic-update-slice_fusion), calls=%async_computation.1 | async-start | bytes 1048576 | tf_op jit(solution)/shard_map/all_to_all | solution.py:75
  28.3 4.1 %copy-start.2 = (bf16[128,4096]{1,0:T(8,128)(2,1)S(1)}, bf16[128,4096]{1,0:T(8,128)(2,1)}, u32[]{:S(2)}) copy-start(bf16[128,4096]{1,0:T(8,128)(2,1)} %param.5) | copy-start | bytes 3145732
  28.5 10.6 %collective-permute-start = (bf16[1025,128]{1,0:T(8,128)(2,1)S(1)}, bf16[1025,128]{1,0:T(8,128)(2,1)S(1)}, u32[]{:S(2)}, u32[]{:S(2)}) collective-permute-start(bf16[1025,128]{1,0:T(8,128)(2,1)S(1)} %get-tuple-element.11), channel_id=1, source_target_pairs={{0,1},{1,2},{2,3},{3,0},{4,5},{5,6},{6,7},{7,4},{8,9},{9,10},{10,1... | collective-permute-start | bytes 787208 | tf_op jit(solution)/shard_map/ppermute | solution.py:17
  30.1 11.2 %collective-permute-start.1 = (bf16[1025,128]{1,0:T(8,128)(2,1)S(1)}, bf16[1025,128]{1,0:T(8,128)(2,1)S(1)}, u32[]{:S(2)}, u32[]{:S(2)}) collective-permute-start(bf16[1025,128]{1,0:T(8,128)(2,1)S(1)} %get-tuple-element.12), channel_id=1, source_target_pairs={{1,0},{2,1},{3,2},{0,3},{5,4},{6,5},{7,6},{4,7},{9,8},{10,9},{11,1... | collective-permute-start | bytes 787208 | tf_op jit(solution)/shard_map/ppermute | solution.py:19
  33.4 23.9 %all-to-all-start = ((bf16[128,8,512]{2,0,1:T(8,128)(2,1)}), bf16[128,8,512]{2,0,1:T(8,128)(2,1)S(1)}, u32[]{:S(2)}, u32[]{:S(2)}) async-start(bf16[128,8,512]{2,0,1:T(8,128)(2,1)} %bitcast.96), calls=%async_computation | async-start | bytes 2097152 | tf_op jit(solution)/shard_map/all_to_all | solution.py:73
  41.5 1.0 copy-start
  57.6 1.2 %copy-start.1 = (bf16[1025,512]{1,0:T(8,128)(2,1)S(1)}, bf16[1025,512]{1,0:T(8,128)(2,1)}, u32[]{:S(2)}) copy-start(bf16[1025,512]{1,0:T(8,128)(2,1)} %copy-done) | copy-start | bytes 3148804
